TPU v7x, 256 devices: a whole 4x4x8 slice. The times are simulated.
256 devices in a mesh: dp: 64 (over x, z, core), tensor: 4 (over y).
Axes of the slice: x: 4, y: 4, z: 8, core: 2. Of those that a mesh axis runs over, the one named last changes fastest.
Arguments:
- activations: bfloat16 [768, 8192], P('dp', 'tensor'), may hold values from -400 to 400, as said below
- weight: bfloat16 [8192, 28672], P('dp', 'tensor'), may hold values from -0.0625 to 0.0625
Outputs:
- channel_mean: float32 [8192], P('dp')
- column_errors: float32 [4, 28672], P(None, ('tensor', 'dp'))
- errors: float32 [4], replicated
Inputs may be any that keep to these rules, and one draw needn't show every extreme that they name: activations and weight are finite real values within the ranges stated above.
All inputs are finite; a program needn't handle non-finite values.
Results may differ from a plain program's by a relative error of at most 0.0012.
The roundings to bfloat16 on the way count: a program that leaves them out, or rounds other values in their place, can miss the bound.
Values may be sent and summed in bfloat16 or wider, within the bound.
A program may use at most 128 MiB of HBM per device.

v0:
```python
import functools
import math

import jax
import jax.numpy as jnp
from jax import lax
from jax.sharding import Mesh
from jax.sharding import PartitionSpec as P

D = 8192
F = 28672
GROUP = 128
GRID = 4
DP = ("dp_0", "dp_1", "dp_2")
DP_TENSOR = ("dp_0", "dp_1", "dp_2", "tensor")
TENSOR_DP = ("tensor", "dp_0", "dp_1", "dp_2")


def laid_out(parts, dim):
    parts = jnp.moveaxis(parts, 0, dim)
    dims = parts.shape
    return parts.reshape(*dims[:dim], dims[dim] * dims[dim + 1], *dims[dim + 2 :])


def from_everyone(shard, axis):
    devices = lax.axis_size(axis)
    return lax.all_to_all(
        jnp.broadcast_to(shard[None], (devices, *shard.shape)), axis, 0, 0, tiled=True
    )


def gather_directly(shard, axis, dim):
    return laid_out(from_everyone(shard, axis), dim)


def by_axis(shard, axes):
    return functools.reduce(lax.psum, axes, shard)


def soft_round(values):
    return values - jnp.sin(2.0 * math.pi * values) / (2.0 * math.pi)


def scale_table(channel_mean):
    ratios = jnp.arange(GRID, dtype=jnp.float32) / GRID
    raw = jnp.exp(ratios[:, None] * jnp.log(channel_mean)[None, :])
    top = jnp.max(raw, axis=1, keepdims=True)
    bottom = jnp.min(raw, axis=1, keepdims=True)
    return raw / jnp.sqrt(top * bottom)


def on_device(activations, weight):
    widened = gather_directly(activations, "tensor", 1)
    gathered = lax.all_gather(widened, DP, axis=0, tiled=True)
    columns = lax.all_to_all(weight, DP, split_axis=1, concat_axis=0, tiled=True)
    width = columns.shape[1]
    token_count = gathered.shape[0]
    channel_mean = jnp.sum(jnp.abs(gathered), axis=0, dtype=jnp.float32) / token_count + 1e-06
    scales = scale_table(channel_mean)
    base_out = jnp.dot(gathered, columns, preferred_element_type=jnp.float32)
    weight_float = columns.astype(jnp.float32)

    def local_error(factor):
        scaled = weight_float * factor[:, None]
        grouped = scaled.reshape(D // GROUP, GROUP, width)
        quant_step = (jnp.max(jnp.abs(grouped), axis=1, keepdims=True) + 1e-06) / 7.0
        levels = soft_round(grouped / quant_step)
        dequant = ((levels * quant_step).reshape(D, width) / factor[:, None]).astype(jnp.bfloat16)
        quant_out = jnp.dot(gathered, dequant, preferred_element_type=jnp.float32)
        residue = quant_out - base_out
        return jnp.sum(residue * residue, axis=0)

    column_sums = lax.map(local_error, scales)
    totals = by_axis(jnp.sum(column_sums, axis=1), DP_TENSOR)
    errors = totals / (token_count * F)
    column_errors = column_sums / token_count
    rows = D // lax.axis_size(DP)
    own_mean = lax.dynamic_slice_in_dim(channel_mean, lax.axis_index(DP) * rows, rows)
    return (own_mean, column_errors, errors)


def solution(mesh):
    torus = Mesh(
        mesh.devices.reshape(4, 8, 2, mesh.shape["tensor"]), ("dp_0", "dp_1", "dp_2", "tensor")
    )
    placed = (P(DP, "tensor"), P(DP, "tensor"))
    return jax.shard_map(
        on_device,
        mesh=torus,
        in_specs=placed,
        out_specs=(P(DP), P(None, TENSOR_DP), P()),
        check_vma=False,
    )
```

profile of v0, /device:TPU:1, one launch (start us, length us, event | category | flops | bytes accessed | tf_op | source)
XLA Modules:
  0.0 333.7 jit_solution(7435003003157472509)
XLA Ops:
  7.2 0.9 broadcast_in_dim.7
  8.1 10.4 %all_to_all.24 = bf16[4,12,2048]{2,1,0:T(8,128)(2,1)S(1)} all-to-all(bf16[4,12,2048]{2,1,0:T(8,128)(2,1)S(1)} %broadcast_in_dim.7), channel_id=1, replica_groups=mesh['dp_0'=4,'dp_1'=8,'dp_2'=2,'tensor'=4] {'tensor'}, dimensions={0} | all-to-all | bytes 393216 | tf_op jit(solution)/shard_map/all_to_all | solution.py:27
  18.6 0.8 reshape.54
  19.4 3.9 %copy.14 = bf16[128,7168]{0,1:T(8,128)(2,1)} copy(bf16[128,7168]{1,0:T(8,128)(2,1)} %param.5) | data formatting | bytes 3670016 | tf_op args[1]
  23.3 13.6 %all-to-all-start.1 = ((bf16[128,64,112]{0,2,1:T(8,128)(2,1)}), bf16[128,64,112]{0,2,1:T(8,128)(2,1)S(1)}, u32[]{:S(2)}, u32[]{:S(2)}) async-start(bf16[128,64,112]{0,2,1:T(8,128)(2,1)} %bitcast.7), calls=%async_computation.1 | async-start | bytes 3670016 | tf_op jit(solution)/shard_map/all_to_all | solution.py:55
  36.9 53.9 %all-to-all-done.1 = bf16[128,64,112]{0,2,1:T(8,128)(2,1)S(1)} async-done(((bf16[128,64,112]{0,2,1:T(8,128)(2,1)}), bf16[128,64,112]{0,2,1:T(8,128)(2,1)S(1)}, u32[]{:S(2)}, u32[]{:S(2)}) %all-to-all-start.1) | async-done | bytes 1835040 | tf_op jit(solution)/shard_map/all_to_all | solution.py:55
  90.8 2.1 bitcast_convert_fusion
  92.9 5.4 %copy.16 = f32[8192,112]{1,0:T(8,128)} copy(f32[8192,112]{0,1:T(8,128)} %bitcast_convert_fusion) | data formatting | bytes 7340032 | tf_op jit(solution)/shard_map/while | solution.py:73
  98.4 35.7 %all-gather.3.cloned.1.call-done = bf16[64,12,8192]{2,1,0:T(8,128)(2,1)} async-done(((bf16[1,12,8192]{2,1,0:T(8,128)(2,1)}), bf16[64,12,8192]{2,1,0:T(8,128)(2,1)}) %all-gather.3.cloned.1.call-update) | async-done | bytes 12582928 | tf_op jit(solution)/shard_map/all_gather | solution.py:54
  134.0 16.8 %reshape.55 = bf16[768,8192]{1,0:T(8,128)(2,1)} reshape(bf16[64,12,8192]{2,1,0:T(8,128)(2,1)} %all-gather.3.cloned.1.call-done) | data formatting | bytes 25165824
  150.9 7.6 %convert_reduce_fusion = f32[8192]{0:T(1024)S(1)} fusion(bf16[768,8192]{1,0:T(8,128)(2,1)} %reshape.55), kind=kLoop, calls=%fused_computation.11 | loop fusion | flops 18866176 | bytes 12615680 | tf_op jit(solution)/shard_map/reduce_sum | solution.py:58
  159.0 8.8 %fusion.5 = f32[768,112]{0,1:T(8,128)S(1)} fusion(bf16[768,8192]{1,0:T(8,128)(2,1)} %reshape.55, bf16[128,64,112]{0,2,1:T(8,128)(2,1)S(1)} %all-to-all-done.1), kind=kOutput, calls=%fused_computation.12 | convolution fusion | flops 1409286144 | bytes 14761984 | tf_op jit(solution)/shard_map/dot_general | solution.py:60
  167.7 122.5 %while.10 = (s32[]{:T(128)}, f32[4,112]{1,0:T(4,128)S(1)}, f32[4,8192]{1,0:T(4,128)S(1)}, f32[8192,112]{1,0:T(8,128)}, bf16[768,8192]{1,0:T(8,128)(2,1)}, /*index=5*/f32[768,112]{0,1:T(8,128)S(1)}, s32[]{:T(128)}, s32[]{:T(128)}) while((s32[]{:T(128)}, f32[4,112]{1,0:T(4,128)S(1)}, f32[4,8192]{1,0:T(4,128)S(1)}, f32[8192,112]{1,0:T(8,128)}, ...), condition=%wide.region_6.7_spmd, body=%wide.region_3.6_spmd.sunk | while | flops 1419643776 | bytes 38864320 | solution.py:73
  168.0 3.2 abs_reduce_fusion.2
  171.4 18.3 %fusion.24 = bf16[8192,112]{1,0:T(8,128)(2,1)S(1)} fusion(f32[8192,112]{1,0:T(8,128)S(1)} %copy-done, f32[64,112]{1,0:T(8,128)S(1)} %add_multiply_fusion.2, f32[8192]{0:T(1024)S(1)} %bitcast.55), kind=kLoop, calls=%fused_computation.3.clone.1 | loop fusion | flops 7340032 | bytes 5566464 | tf_op jit(solution)/shard_map/while/body/eval_jaxpr/convert_element_type | solution.py:68
  189.7 8.8 %fusion.25 = f32[112]{0:T(128)S(1)} fusion(f32[768,112]{0,1:T(8,128)S(1)} %get-tuple-element.130, bf16[8192,112]{1,0:T(8,128)(2,1)S(1)} %fusion.24, bf16[768,8192]{1,0:T(8,128)(2,1)} %get-tuple-element.129), kind=kOutput, calls=%fused_computation.8.clone.1 | convolution fusion | flops 1409544064 | bytes 14762432 | tf_op jit(solution)/shard_map/while/body/eval_jaxpr/dot_general | solution.py:69
  198.6 3.2 abs_reduce_fusion.2
  202.0 18.3 %fusion.24 = bf16[8192,112]{1,0:T(8,128)(2,1)S(1)} fusion(f32[8192,112]{1,0:T(8,128)S(1)} %copy-done, f32[64,112]{1,0:T(8,128)S(1)} %add_multiply_fusion.2, f32[8192]{0:T(1024)S(1)} %bitcast.55), kind=kLoop, calls=%fused_computation.3.clone.1 | loop fusion | flops 7340032 | bytes 5566464 | tf_op jit(solution)/shard_map/while/body/eval_jaxpr/convert_element_type | solution.py:68
  220.2 8.8 %fusion.25 = f32[112]{0:T(128)S(1)} fusion(f32[768,112]{0,1:T(8,128)S(1)} %get-tuple-element.130, bf16[8192,112]{1,0:T(8,128)(2,1)S(1)} %fusion.24, bf16[768,8192]{1,0:T(8,128)(2,1)} %get-tuple-element.129), kind=kOutput, calls=%fused_computation.8.clone.1 | convolution fusion | flops 1409544064 | bytes 14762432 | tf_op jit(solution)/shard_map/while/body/eval_jaxpr/dot_general | solution.py:69
  229.1 3.2 abs_reduce_fusion.2
  232.5 18.3 %fusion.24 = bf16[8192,112]{1,0:T(8,128)(2,1)S(1)} fusion(f32[8192,112]{1,0:T(8,128)S(1)} %copy-done, f32[64,112]{1,0:T(8,128)S(1)} %add_multiply_fusion.2, f32[8192]{0:T(1024)S(1)} %bitcast.55), kind=kLoop, calls=%fused_computation.3.clone.1 | loop fusion | flops 7340032 | bytes 5566464 | tf_op jit(solution)/shard_map/while/body/eval_jaxpr/convert_element_type | solution.py:68
  250.8 8.8 %fusion.25 = f32[112]{0:T(128)S(1)} fusion(f32[768,112]{0,1:T(8,128)S(1)} %get-tuple-element.130, bf16[8192,112]{1,0:T(8,128)(2,1)S(1)} %fusion.24, bf16[768,8192]{1,0:T(8,128)(2,1)} %get-tuple-element.129), kind=kOutput, calls=%fused_computation.8.clone.1 | convolution fusion | flops 1409544064 | bytes 14762432 | tf_op jit(solution)/shard_map/while/body/eval_jaxpr/dot_general | solution.py:69
  259.7 3.2 abs_reduce_fusion.2
  263.1 18.3 %fusion.24 = bf16[8192,112]{1,0:T(8,128)(2,1)S(1)} fusion(f32[8192,112]{1,0:T(8,128)S(1)} %copy-done, f32[64,112]{1,0:T(8,128)S(1)} %add_multiply_fusion.2, f32[8192]{0:T(1024)S(1)} %bitcast.55), kind=kLoop, calls=%fused_computation.3.clone.1 | loop fusion | flops 7340032 | bytes 5566464 | tf_op jit(solution)/shard_map/while/body/eval_jaxpr/convert_element_type | solution.py:68
  281.4 8.8 %fusion.25 = f32[112]{0:T(128)S(1)} fusion(f32[768,112]{0,1:T(8,128)S(1)} %get-tuple-element.130, bf16[8192,112]{1,0:T(8,128)(2,1)S(1)} %fusion.24, bf16[768,8192]{1,0:T(8,128)(2,1)} %get-tuple-element.129), kind=kOutput, calls=%fused_computation.8.clone.1 | convolution fusion | flops 1409544064 | bytes 14762432 | tf_op jit(solution)/shard_map/while/body/eval_jaxpr/dot_general | solution.py:69
  290.2 0.7 fusion.12
  290.9 6.5 %psum.28 = f32[4]{0:T(128)S(1)} all-reduce(f32[4]{0:T(128)S(1)} %get-tuple-element.70), channel_id=1, replica_groups=mesh['dp_0'=4,'dp_1'=8,'dp_2'=2,'tensor'=4] {'dp_0'}, use_global_device_ids=true, to_apply=%region_8.9 | all-reduce | flops 4 | bytes 32 | tf_op jit(solution)/shard_map/psum | solution.py:37
  297.4 12.1 %psum.29 = f32[4]{0:T(128)S(1)} all-reduce(f32[4]{0:T(128)S(1)} %psum.28), channel_id=1, replica_groups=mesh['dp_0'=4,'dp_1'=8,'dp_2'=2,'tensor'=4] {'dp_1'}, use_global_device_ids=true, to_apply=%region_9.10 | all-reduce | flops 4 | bytes 32 | tf_op jit(solution)/shard_map/psum | solution.py:37
  309.5 8.1 %psum.30 = f32[4]{0:T(128)S(1)} all-reduce(f32[4]{0:T(128)S(1)} %psum.29), channel_id=1, replica_groups=mesh['dp_0'=4,'dp_1'=8,'dp_2'=2,'tensor'=4] {'dp_2'}, use_global_device_ids=true, to_apply=%region_10.11 | all-reduce | flops 4 | bytes 32 | tf_op jit(solution)/shard_map/psum | solution.py:37
  317.6 8.1 %psum.31 = f32[4]{0:T(128)S(1)} all-reduce(f32[4]{0:T(128)S(1)} %psum.30), channel_id=1, replica_groups=mesh['dp_0'=4,'dp_1'=8,'dp_2'=2,'tensor'=4] {'tensor'}, use_global_device_ids=true, to_apply=%region_11.12 | all-reduce | flops 4 | bytes 32 | tf_op jit(solution)/shard_map/psum | solution.py:37
  325.8 0.5 broadcast_multiply_fusion.1
  326.3 0.6 dynamic_slice.7
  (29 shorter events, 1.8 us)
Async XLA Ops:
  7.2 126.9 %all-gather.3.cloned.1.call-start = ((), (), s32[]{:S(2)}) async-start(), calls=%async_computation.2 | async-start | bytes 17039360 | tf_op jit(solution)/shard_map/all_gather | solution.py:54
  23.3 67.5 %all-to-all-start.1 = ((bf16[128,64,112]{0,2,1:T(8,128)(2,1)}), bf16[128,64,112]{0,2,1:T(8,128)(2,1)S(1)}, u32[]{:S(2)}, u32[]{:S(2)}) async-start(bf16[128,64,112]{0,2,1:T(8,128)(2,1)} %bitcast.7), calls=%async_computation.1 | async-start | bytes 3670016 | tf_op jit(solution)/shard_map/all_to_all | solution.py:55
  167.9 3.5 %copy-start = (f32[8192,112]{1,0:T(8,128)S(1)}, f32[8192,112]{1,0:T(8,128)}, u32[]{:S(2)}) copy-start(f32[8192,112]{1,0:T(8,128)} %get-tuple-element.128) | copy-start | bytes 11010052 | tf_op jit(solution)/shard_map/while
  198.5 3.5 %copy-start = (f32[8192,112]{1,0:T(8,128)S(1)}, f32[8192,112]{1,0:T(8,128)}, u32[]{:S(2)}) copy-start(f32[8192,112]{1,0:T(8,128)} %get-tuple-element.128) | copy-start | bytes 11010052 | tf_op jit(solution)/shard_map/while
  229.1 3.5 %copy-start = (f32[8192,112]{1,0:T(8,128)S(1)}, f32[8192,112]{1,0:T(8,128)}, u32[]{:S(2)}) copy-start(f32[8192,112]{1,0:T(8,128)} %get-tuple-element.128) | copy-start | bytes 11010052 | tf_op jit(solution)/shard_map/while
  259.7 3.5 %copy-start = (f32[8192,112]{1,0:T(8,128)S(1)}, f32[8192,112]{1,0:T(8,128)}, u32[]{:S(2)}) copy-start(f32[8192,112]{1,0:T(8,128)} %get-tuple-element.128) | copy-start | bytes 11010052 | tf_op jit(solution)/shard_map/while
Sparse Core Ops, SparseCore 0:
  19.5 114.4 all-gather.2
where the time goes:
time: 335 us; the launch traced here: 334 us
  other arithmetic  97.2 us (29%)
  waiting for transfers between devices  89.5 us (27%)
  blocking collectives  45.2 us (13%)
  matrix products  44 us (13%)
  local copies, waits for them, and re-layouts  29.7 us (9%)
  between operations  14.1 us (4%)
  starting transfers between devices  13.6 us (4%)
    convert_element_type x4, other arithmetic, local_error(): ((levels * quant_step).reshape(D, width) / factor[:, None]).astype(jnp.bf...  73 us
    all_to_all x1, waiting for transfers between devices, on_device(): lax.all_to_all(weight, DP, split_axis=1, concat_axis=0, tiled=True)  53.9 us
    all_gather x1, waiting for transfers between devices, on_device(): gathered = lax.all_gather(widened, DP, axis=0, tiled=True)  35.7 us
    dot_general x4, matrix products, local_error(): quant_out = jnp.dot(gathered, dequant, preferred_element_type=jnp.float32)  35.2 us
    psum x4, blocking collectives, by_axis(): return functools.reduce(lax.psum, axes, shard)  34.9 us
    unnamed x3, local copies, waits for them, and re-layouts  21.6 us
    all_to_all x1, starting transfers between devices, on_device(): lax.all_to_all(weight, DP, split_axis=1, concat_axis=0, tiled=True)  13.6 us
    reduce_max x4, other arithmetic, local_error(): jnp.max(jnp.abs(grouped), axis=1, keepdims=True) + 1e-06  12.7 us
  transfers between devices with their start and end apart: 2, of which 2 were waited for; matrix products, arithmetic and copies ran while one was open for 3% of the time, Pallas kernels for 0%

commit v1 on v0

v1 whole, which is shorter than its diff:
```python
import functools

import jax
import jax.numpy as jnp
from jax import lax
from jax.experimental import pallas as pl
from jax.experimental.pallas import tpu as pltpu
from jax.sharding import Mesh
from jax.sharding import PartitionSpec as P

D = 8192
F = 28672
GROUP = 128
GRID = 4
TOKENS = 768
NX, NZ, NC, NY = 4, 8, 2, 4
PLANE = NX * NZ
ACTIVE = 28
ROWS = 24
HALF = 1024
WIDE = 256
SUB = HALF // GROUP
DP = ("x", "z", "c")
Z_ORDER = (0, -1, 1, -2, 2, -3, 3, -4)
WAVE = (6.579736255173805, -12.987875283620534, 12.207951996649596, -6.691021837978725, 2.380346767313312, -0.5278301996489366)
MESH_ID = pl.DeviceIdType.MESH


def kernel(
    act, w, mean_out, cols_out, errors_out,
    swap, abuf, dbuf, acc, part, other, stat, staty, ends, table, inverse, tiles, mine, finals, finaly, finalc,
    send_small, send_piece, send_w, send_part,
    swap_sem, z_sem, xl_sem, xr_sem, x2_sem, yd_sem, yu_sem, y2_sem, w_sem, stat_sem, staty_sem, ends_sem,
    part_sem, tile_sem, fin_sem, finy_sem, finc_sem, own_sem,
):
    x, z, c, y = (lax.axis_index(name) for name in ("x", "z", "c", "y"))
    me = x * NZ + z
    active = me < ACTIVE

    def device(dx=0, dz=0, dc=0, dy=0):
        return {
            "x": lax.rem(x + dx + NX, NX),
            "z": lax.rem(z + dz + NZ, NZ),
            "c": lax.rem(c + dc, NC),
            "y": lax.rem(y + dy + NY, NY),
        }

    def remote(src, dst, send, recv, to):
        return pltpu.make_async_remote_copy(
            src_ref=src, dst_ref=dst, send_sem=send, recv_sem=recv, device_id=to, device_id_type=MESH_ID
        )

    def arrived(ref, sem):
        pltpu.make_async_copy(ref, ref, sem).wait()

    barrier = pltpu.get_barrier_semaphore()

    def greet(n, _):
        to = device(n // (NZ * NC), lax.rem(n // NC, NZ), lax.rem(n, NC))
        pl.semaphore_signal(barrier, inc=1, device_id=to, device_id_type=MESH_ID)
        return 0

    lax.fori_loop(1, PLANE * NC, greet, 0)
    for dy in range(1, NY):
        pl.semaphore_signal(barrier, inc=1, device_id=device(dy=dy), device_id_type=MESH_ID)
    pl.semaphore_wait(barrier, PLANE * NC - 1 + NY - 1)

    def lanes(group):
        return pl.ds(pl.multiple_of(group * GROUP, GROUP), GROUP)

    for j in range(SUB):
        remote(
            act.at[:, lanes(2 * j + 1 - c)], swap.at[j], send_small.at[0], swap_sem.at[j], device(dc=1)
        ).start()
    here = c == 0
    for j in range(SUB):
        arrived(swap.at[j], swap_sem.at[j])
        own = act[:, lanes(2 * j + c)].astype(jnp.float32)
        peer = swap[j].astype(jnp.float32)
        block = jnp.concatenate([jnp.where(here, own, peer), jnp.where(here, peer, own)], axis=0)
        stat[me, j : j + 1, :] = jnp.sum(jnp.abs(block), axis=0, keepdims=True)
        abuf[y, me, :, j * GROUP : (j + 1) * GROUP] = block.astype(jnp.bfloat16)

    def send_stat(n, _):
        to = device(n // NZ, lax.rem(n, NZ))
        remote(stat.at[me], stat.at[me], send_small.at[1], stat_sem.at[me], to).start()
        return 0

    lax.fori_loop(1, PLANE, send_stat, 0)

    def send_weight(dx, dz):
        to = device(dx, dz)
        there = to["x"] * NZ + to["z"]

        @pl.when(there < ACTIVE)
        def _():
            columns = w.at[:, pl.ds(pl.multiple_of(there * WIDE, WIDE), WIDE)]
            if dx == 0 and dz == 0:
                pltpu.make_async_copy(columns, dbuf.at[GRID, me], own_sem.at[0]).start()
            else:
                remote(columns, dbuf.at[GRID, me], send_w.at[0], w_sem.at[me], to).start()

    def along(index):
        return lax.rem(z + index + NZ, NZ)

    def piece(yy, xx, k):
        return abuf.at[lax.rem(yy + NY, NY), lax.rem(xx + NX, NX) * NZ + along(Z_ORDER[k])]

    def pass_on(ref, sem, **to):
        remote(ref, ref, send_piece.at[0], sem, device(**to)).start()

    def up_and_down(ref, n):
        pass_on(ref, yd_sem.at[n], dy=1)
        pass_on(ref, yu_sem.at[n], dy=-1)

    for k in range(NZ):
        ref = piece(y, x, k)
        if k > 0:
            arrived(ref, z_sem.at[k])
        if k == 0 or (k % 2 == 1 and k < 7):
            pass_on(ref, z_sem.at[k + 1 if k == 0 else k + 2], dz=1)
        if k == 0 or (k % 2 == 0 and k < 6):
            pass_on(ref, z_sem.at[k + 2], dz=-1)
        pass_on(ref, xl_sem.at[k], dx=1)
        pass_on(ref, xr_sem.at[k], dx=-1)
        up_and_down(ref, k)
        for dx in (2, 1, 3, 0):
            send_weight(dx, Z_ORDER[7 - k])

    def hear_stat(n, _):
        there = lax.rem(x + n // NZ, NX) * NZ + lax.rem(z + lax.rem(n, NZ), NZ)
        arrived(stat.at[there], stat_sem.at[there])
        return 0

    lax.fori_loop(1, PLANE, hear_stat, 0)
    staty[y] = jnp.sum(stat[...], axis=0)
    for dy in range(1, NY):
        remote(staty.at[y], staty.at[y], send_small.at[1], staty_sem.at[y], device(dy=dy)).start()

    for k in range(NZ):
        left, right = piece(y, x - 1, k), piece(y, x + 1, k)
        arrived(left, xl_sem.at[k])
        if k < 4:
            pass_on(left, x2_sem.at[k], dx=1)
        up_and_down(left, 8 + 2 * k)
        arrived(right, xr_sem.at[k])
        if k >= 4:
            pass_on(right, x2_sem.at[k], dx=-1)
        up_and_down(right, 9 + 2 * k)

    for dy in range(1, NY):
        there = lax.rem(y + dy, NY)
        arrived(staty.at[there], staty_sem.at[there])
    channel_mean = staty[...].reshape(PLANE, GROUP) / TOKENS + 1e-06
    own_mean = staty[x, pl.ds(z, 1), :] / TOKENS + 1e-06
    mean_out[...] = own_mean
    log_mean = jnp.log(channel_mean)
    ends[c, 0] = jnp.broadcast_to(jnp.max(log_mean, axis=0, keepdims=True), (8, GROUP))
    ends[c, 1] = jnp.broadcast_to(jnp.min(log_mean, axis=0, keepdims=True), (8, GROUP))
    remote(ends.at[c], ends.at[c], send_small.at[2], ends_sem.at[0], device(dc=1)).start()
    for k in range(NZ):
        far = piece(y, x + 2, k)
        arrived(far, x2_sem.at[k])
        up_and_down(far, 24 + k)
    arrived(ends.at[1 - c], ends_sem.at[0])
    top = jnp.max(jnp.maximum(ends[0, 0], ends[1, 0]), axis=(0, 1), keepdims=True)
    bottom = jnp.min(jnp.minimum(ends[0, 1], ends[1, 1]), axis=(0, 1), keepdims=True)
    rows = []
    for k in range(1, GRID):
        ratio = k / GRID
        level = jnp.sqrt(jnp.exp(ratio * top) * jnp.exp(ratio * bottom))
        rows.append(jnp.exp(ratio * log_mean) / level)
    rows.append(jnp.ones((PLANE, GROUP), jnp.float32))
    stacked = jnp.concatenate(rows, axis=0)
    table[...] = stacked.T
    inverse[...] = (1.0 / stacked).T

    def quantize(slot):
        weight = dbuf[GRID, slot].astype(jnp.float32)
        factors = pltpu.roll(table[...], GROUP - slot, 1)
        backs = pltpu.roll(inverse[...], GROUP - slot, 1)
        for k in range(GRID):
            if k == 0:
                scaled = weight
            else:
                at = (k - 1) * PLANE
                scaled = weight * factors[:, at : at + 1]
            step = (jnp.max(jnp.abs(scaled), axis=0, keepdims=True) + 1e-06) * (1.0 / 7.0)
            value = scaled * (1.0 / step)
            whole = jnp.round(value)
            rest = value - whole
            square = rest * rest
            wave = jnp.full_like(square, WAVE[-1])
            for term in WAVE[-2::-1]:
                wave = wave * square + term
            level = whole + rest * square * wave
            result = level * step
            if k > 0:
                result = result * backs[:, at : at + 1]
            dbuf[k, slot] = result.astype(jnp.bfloat16)

    def relay(n, _):
        xx, zz = x, z
        order = jnp.where(n < 8, n, jnp.where(n < 24, (n - 8) // 2, n - 24))
        dx = jnp.where(n < 8, 0, jnp.where(n < 24, jnp.where(lax.rem(n, 2) == 0, -1, 1), 2))
        dz = jnp.where(lax.rem(order, 2) == 1, -((order + 1) // 2), order // 2)
        slot = lax.rem(xx + dx + NX, NX) * NZ + lax.rem(zz + dz + NZ, NZ)
        below = abuf.at[lax.rem(y + NY - 1, NY), slot]
        above = abuf.at[lax.rem(y + 1, NY), slot]
        arrived(below, yd_sem.at[n])

        @pl.when(lax.rem(n, 2) == 0)
        def _():
            pass_on(below, y2_sem.at[n], dy=1)

        arrived(above, yu_sem.at[n])

        @pl.when(lax.rem(n, 2) == 1)
        def _():
            pass_on(above, y2_sem.at[n], dy=-1)

        @pl.when(active)
        def _():
            @pl.when(slot == me)
            def _():
                pltpu.make_async_copy(dbuf.at[GRID, slot], dbuf.at[GRID, slot], own_sem.at[0]).wait()

            @pl.when(slot != me)
            def _():
                arrived(dbuf.at[GRID, slot], w_sem.at[slot])

            quantize(slot)

        return 0

    lax.fori_loop(0, PLANE, relay, 0)

    def last(n, _):
        order = jnp.where(n < 8, n, jnp.where(n < 24, (n - 8) // 2, n - 24))
        dx = jnp.where(n < 8, 0, jnp.where(n < 24, jnp.where(lax.rem(n, 2) == 0, -1, 1), 2))
        dz = jnp.where(lax.rem(order, 2) == 1, -((order + 1) // 2), order // 2)
        slot = lax.rem(x + dx + NX, NX) * NZ + lax.rem(z + dz + NZ, NZ)
        arrived(abuf.at[lax.rem(y + 2, NY), slot], y2_sem.at[n])
        return 0

    lax.fori_loop(0, PLANE, last, 0)

    @pl.when(active)
    def _():
        def multiply(n, _):
            block, k = n // (GRID + 1), lax.rem(n, GRID + 1)
            lhs = abuf[block].reshape(TOKENS, HALF)
            rhs = dbuf[k, pl.ds(block * SUB, SUB)].reshape(HALF, WIDE)
            product = jnp.dot(lhs, rhs, preferred_element_type=jnp.float32)

            @pl.when(block == 0)
            def _():
                acc[k] = product

            @pl.when(block > 0)
            def _():
                acc[k] += product

            return 0

        lax.fori_loop(0, NY * (GRID + 1), multiply, 0)
        for k in range(GRID):
            residue = acc[k] - acc[GRID]
            part[k, 0] = residue[:, :GROUP]
            part[k, 1] = residue[:, GROUP:]
            remote(part.at[k, 1 - c], other.at[k], send_part.at[0], part_sem.at[k], device(dc=1)).start()
        sums = []
        for k in range(GRID):
            arrived(other.at[k], part_sem.at[k])
            residue = part[k, c] + other[k]
            sums.append(jnp.sum(residue * residue, axis=0, keepdims=True))
        mine[...] = jnp.concatenate(sums + [jnp.zeros((GRID, GROUP), jnp.float32)], axis=0)

    @pl.when(jnp.logical_not(active))
    def _():
        mine[...] = jnp.zeros((8, GROUP), jnp.float32)

    tile = 2 * me + c
    owner = (tile // 7) * 8 + lax.rem(tile, 7)

    def send_tile(to_index, slot):
        to = {"x": to_index // (NZ * NC), "z": lax.rem(to_index // NC, NZ), "c": lax.rem(to_index, NC), "y": y}
        same = to_index == tile

        @pl.when(jnp.logical_not(same))
        def _():
            remote(mine, tiles.at[slot], send_small.at[3], tile_sem.at[slot], to).start()

        @pl.when(same)
        def _():
            tiles[slot] = mine[...]

    @pl.when(active)
    def _():
        send_tile(owner, 1)
        send_tile(owner + 1, 0)

    finals[me] = mine[...]

    def send_final(n, _):
        remote(finals.at[me], finals.at[me], send_small.at[4], fin_sem.at[me], device(n // NZ, lax.rem(n, NZ))).start()
        return 0

    lax.fori_loop(1, PLANE, send_final, 0)

    place = lax.rem(tile, 8)
    before = (tile // 8) * 7 + place - 1
    after = before + 1

    @pl.when(jnp.logical_and(place > 0, before != tile))
    def _():
        arrived(tiles.at[0], tile_sem.at[0])

    @pl.when(place == 0)
    def _():
        tiles[0] = jnp.zeros((8, GROUP), jnp.float32)

    @pl.when(jnp.logical_and(place < 7, after != tile))
    def _():
        arrived(tiles.at[1], tile_sem.at[1])

    @pl.when(place == 7)
    def _():
        tiles[1] = jnp.zeros((8, GROUP), jnp.float32)

    shift = 16 * place
    lane = lax.broadcasted_iota(jnp.int32, (8, GROUP), 1)
    joined = jnp.where(lane < shift, pltpu.roll(tiles[0], shift, 1), pltpu.roll(tiles[1], shift, 1))
    cols_out[...] = joined / TOKENS

    def hear_final(n, _):
        there = lax.rem(x + n // NZ, NX) * NZ + lax.rem(z + lax.rem(n, NZ), NZ)
        arrived(finals.at[there], fin_sem.at[there])
        return 0

    lax.fori_loop(1, PLANE, hear_final, 0)
    finaly[y] = jnp.sum(finals[...], axis=0)
    for dy in range(1, NY):
        remote(finaly.at[y], finaly.at[y], send_small.at[4], finy_sem.at[y], device(dy=dy)).start()
    for dy in range(1, NY):
        there = lax.rem(y + dy, NY)
        arrived(finaly.at[there], finy_sem.at[there])
    finalc[c] = jnp.sum(finaly[...], axis=0)
    remote(finalc.at[c], finalc.at[c], send_small.at[4], finc_sem.at[0], device(dc=1)).start()
    arrived(finalc.at[1 - c], finc_sem.at[0])
    total = jnp.sum(finalc[0] + finalc[1], axis=1, keepdims=True)
    errors_out[...] = jnp.broadcast_to(total / (TOKENS * F), (8, GROUP))

    for j in range(SUB):
        arrived(swap.at[j], send_small.at[0])

    def left_stat(n, _):
        arrived(stat.at[0], send_small.at[1])
        return 0

    lax.fori_loop(0, PLANE - 1 + NY - 1, left_stat, 0)
    arrived(ends.at[0], send_small.at[2])

    @pl.when(active)
    def _():
        @pl.when(owner != tile)
        def _():
            arrived(mine, send_small.at[3])

        @pl.when(owner + 1 != tile)
        def _():
            arrived(mine, send_small.at[3])

        for k in range(GRID):
            arrived(other.at[0], send_part.at[0])

    def left_final(n, _):
        arrived(finals.at[0], send_small.at[4])
        return 0

    lax.fori_loop(0, PLANE - 1 + NY - 1 + 1, left_final, 0)

    def left_piece(n, _):
        arrived(abuf.at[0, 0], send_piece.at[0])
        return 0

    lax.fori_loop(0, NZ - 1 + 2 * NZ + NZ + 2 * PLANE + PLANE, left_piece, 0)

    def left_weight(n, _):
        arrived(dbuf.at[GRID, 0], send_w.at[0])
        return 0

    lax.fori_loop(0, jnp.where(active, ACTIVE - 1, ACTIVE), left_weight, 0)


def on_device(activations, weight):
    vmem = pl.BlockSpec(memory_space=pltpu.VMEM)
    dma = pltpu.SemaphoreType.DMA
    f32, bf16 = jnp.float32, jnp.bfloat16
    own_mean, cols, errors = pl.pallas_call(
        kernel,
        out_shape=(
            jax.ShapeDtypeStruct((1, GROUP), f32),
            jax.ShapeDtypeStruct((8, GROUP), f32),
            jax.ShapeDtypeStruct((8, GROUP), f32),
        ),
        in_specs=[vmem, pl.BlockSpec(memory_space=pl.ANY)],
        out_specs=(vmem, vmem, vmem),
        scratch_shapes=[
            pltpu.VMEM((SUB, ROWS // 2, GROUP), bf16),
            pltpu.VMEM((NY, PLANE, ROWS, HALF), bf16),
            pltpu.VMEM((GRID + 1, PLANE, GROUP, WIDE), bf16),
            pltpu.VMEM((GRID + 1, TOKENS, WIDE), f32),
            pltpu.VMEM((GRID, NC, TOKENS, GROUP), f32),
            pltpu.VMEM((GRID, TOKENS, GROUP), f32),
            pltpu.VMEM((PLANE, 8, GROUP), f32),
            pltpu.VMEM((NY, 8, GROUP), f32),
            pltpu.VMEM((NC, 2, 8, GROUP), f32),
            pltpu.VMEM((GROUP, GROUP), f32),
            pltpu.VMEM((GROUP, GROUP), f32),
            pltpu.VMEM((2, 8, GROUP), f32),
            pltpu.VMEM((8, GROUP), f32),
            pltpu.VMEM((PLANE, 8, GROUP), f32),
            pltpu.VMEM((NY, 8, GROUP), f32),
            pltpu.VMEM((NC, 8, GROUP), f32),
            dma((5,)),
            dma((1,)),
            dma((1,)),
            dma((1,)),
            dma((SUB,)),
            dma((NZ,)),
            dma((NZ,)),
            dma((NZ,)),
            dma((NZ,)),
            dma((PLANE,)),
            dma((PLANE,)),
            dma((PLANE,)),
            dma((PLANE,)),
            dma((PLANE,)),
            dma((NY,)),
            dma((1,)),
            dma((GRID,)),
            dma((2,)),
            dma((PLANE,)),
            dma((NY,)),
            dma((1,)),
            dma((1,)),
        ],
        compiler_params=pltpu.CompilerParams(
            collective_id=0, has_side_effects=True, vmem_limit_bytes=60 * 1024 * 1024
        ),
    )(activations, weight)
    return own_mean[0], cols[:GRID, :112], errors[:GRID, 0]


def solution(mesh):
    torus = Mesh(mesh.devices.reshape(NX, NZ, NC, NY), ("x", "z", "c", "y"))
    placed = (P(DP, "y"), P(DP, "y"))
    return jax.shard_map(
        on_device,
        mesh=torus,
        in_specs=placed,
        out_specs=(P(DP), P(None, ("y", "x", "z", "c")), P()),
        check_vma=False,
    )
```

time: 335 us -> 141 us (0.42)
  Pallas kernels: 0 us -> 137 us
  other arithmetic: 97.2 us -> 0 us
  waiting for transfers between devices: 89.5 us -> 0 us
  blocking collectives: 45.2 us -> 0 us
  matrix products: 44 us -> 0 us
  local copies, waits for them, and re-layouts: 29.7 us -> 3.69 us
  starting transfers between devices: 13.6 us -> 0 us
  between operations: 14.1 us -> 0.64 us
    pallas_call x0 -> x1, Pallas kernels: none -> 137 us  [on_device(): pl.pallas_call(kernel, out_shape=(jax.ShapeDtypeStruct((1, GROUP), f32),...]
    convert_element_type x5 -> x0, other arithmetic: 75.2 us -> none  [the longest x4 73 us: local_error(): ((levels * quant_step).reshape(D, width) / factor[:, None]).astype(jnp.bf...]
    all_to_all x1 -> x0, waiting for transfers between devices: 53.9 us -> none  [on_device(): lax.all_to_all(weight, DP, split_axis=1, concat_axis=0, tiled=True)]
    dot_general x5 -> x0, matrix products: 44 us -> none  [the longest x4 35.2 us: local_error(): quant_out = jnp.dot(gathered, dequant, preferred_element_type=jnp.float32)]
    all_gather x1 -> x0, waiting for transfers between devices: 35.7 us -> none  [on_device(): gathered = lax.all_gather(widened, DP, axis=0, tiled=True)]
    psum x4 -> x0, blocking collectives: 34.9 us -> none  [by_axis(): return functools.reduce(lax.psum, axes, shard)]
    unnamed x3 -> x1, local copies, waits for them, and re-layouts: 21.6 us -> 1.14 us
    all_to_all x1 -> x0, starting transfers between devices: 13.6 us -> none  [on_device(): lax.all_to_all(weight, DP, split_axis=1, concat_axis=0, tiled=True)]
  transfers between devices with their start and end apart: 2 -> 0, of which waited for: 2 -> 0; matrix products, arithmetic and copies ran while one was open for 3% -> 0% of each run, Pallas kernels for 0% -> 0%
where the time goes in v1:
time: 141 us
  Pallas kernels  137 us (97%)
  local copies, waits for them, and re-layouts  3.69 us (3%)
    pallas_call x1, Pallas kernels, on_device(): pl.pallas_call(kernel, out_shape=(jax.ShapeDtypeStruct((1, GROUP), f32),...  137 us

profile of v1, /device:TPU:1, one launch (start us, length us, event | category | flops | bytes accessed | tf_op | source)
XLA Modules:
  0.0 141.0 jit_solution(2389011782691291321)
XLA Ops:
  0.6 136.7 %shard_map.49 = (f32[1,128]{1,0:T(1,128)}, f32[8,128]{1,0:T(8,128)}, f32[8,128]{1,0:T(8,128)}) custom-call(bf16[12,2048]{1,0:T(8,128)(2,1)} %act.1, bf16[128,7168]{1,0:T(8,128)(2,1)} %w.1), custom_call_target="tpu_custom_call" | custom-call | tf_op jit(solution)/shard_map/pallas_call | solution.py:400
  137.3 1.3 slice_reduce_fusion
  138.6 1.3 slice.6
  139.9 1.1 copy.6

commit v2 on v1

--- a/solution.py
+++ b/solution.py
@@ -22,16 +22,27 @@
 SUB = HALF // GROUP
 DP = ("x", "z", "c")
 Z_ORDER = (0, -1, 1, -2, 2, -3, 3, -4)
+X_ORDER = (0, 3, 1, 2)
 WAVE = (6.579736255173805, -12.987875283620534, 12.207951996649596, -6.691021837978725, 2.380346767313312, -0.5278301996489366)
+EARLY = (
+    (),
+    ((0, -4),),
+    ((0, 3),),
+    ((0, -3),),
+    (),
+    ((0, 2),),
+    ((0, -2),),
+    ((0, 1), (0, -1), (0, 0)),
+)
 MESH_ID = pl.DeviceIdType.MESH
 
 
 def kernel(
     act, w, mean_out, cols_out, errors_out,
-    swap, abuf, dbuf, acc, part, other, stat, staty, ends, table, inverse, tiles, mine, finals, finaly, finalc,
+    swap, abuf, dbuf, acc, part, other, stat, staty, ends, table, inverse, tiles, mine, finals, finaly,
     send_small, send_piece, send_w, send_part,
     swap_sem, z_sem, xl_sem, xr_sem, x2_sem, yd_sem, yu_sem, y2_sem, w_sem, stat_sem, staty_sem, ends_sem,
-    part_sem, tile_sem, fin_sem, finy_sem, finc_sem, own_sem,
+    part_sem, tile_sem, fin_sem, finy_sem, own_sem,
 ):
     x, z, c, y = (lax.axis_index(name) for name in ("x", "z", "c", "y"))
     me = x * NZ + z
@@ -62,8 +73,11 @@
 
     lax.fori_loop(1, PLANE * NC, greet, 0)
     for dy in range(1, NY):
-        pl.semaphore_signal(barrier, inc=1, device_id=device(dy=dy), device_id_type=MESH_ID)
-    pl.semaphore_wait(barrier, PLANE * NC - 1 + NY - 1)
+        for dc in range(NC):
+            pl.semaphore_signal(barrier, inc=1, device_id=device(dy=dy, dc=dc), device_id_type=MESH_ID)
+    for k in range(GRID + 1):
+        acc[k] = jnp.zeros((TOKENS, WIDE), jnp.float32)
+    pl.semaphore_wait(barrier, PLANE * NC - 1 + (NY - 1) * NC)
 
     def lanes(group):
         return pl.ds(pl.multiple_of(group * GROUP, GROUP), GROUP)
@@ -88,13 +102,19 @@
 
     lax.fori_loop(1, PLANE, send_stat, 0)
 
+    def columns_of(there):
+        return w.at[:, pl.ds(pl.multiple_of(there * WIDE, WIDE), WIDE)]
+
+    def index_of(to):
+        return to["x"] * NZ + to["z"]
+
     def send_weight(dx, dz):
         to = device(dx, dz)
-        there = to["x"] * NZ + to["z"]
+        there = index_of(to)
 
         @pl.when(there < ACTIVE)
         def _():
-            columns = w.at[:, pl.ds(pl.multiple_of(there * WIDE, WIDE), WIDE)]
+            columns = columns_of(there)
             if dx == 0 and dz == 0:
                 pltpu.make_async_copy(columns, dbuf.at[GRID, me], own_sem.at[0]).start()
             else:
@@ -124,8 +144,8 @@
         pass_on(ref, xl_sem.at[k], dx=1)
         pass_on(ref, xr_sem.at[k], dx=-1)
         up_and_down(ref, k)
-        for dx in (2, 1, 3, 0):
-            send_weight(dx, Z_ORDER[7 - k])
+        for item in EARLY[k]:
+            send_weight(*item)
 
     def hear_stat(n, _):
         there = lax.rem(x + n // NZ, NX) * NZ + lax.rem(z + lax.rem(n, NZ), NZ)
@@ -147,6 +167,10 @@
         if k >= 4:
             pass_on(right, x2_sem.at[k], dx=-1)
         up_and_down(right, 9 + 2 * k)
+        send_weight(2, Z_ORDER[7 - k])
+    for k in range(NZ):
+        send_weight(3, Z_ORDER[7 - k])
+        send_weight(1, Z_ORDER[7 - k])
 
     for dy in range(1, NY):
         there = lax.rem(y + dy, NY)
@@ -158,10 +182,6 @@
     ends[c, 0] = jnp.broadcast_to(jnp.max(log_mean, axis=0, keepdims=True), (8, GROUP))
     ends[c, 1] = jnp.broadcast_to(jnp.min(log_mean, axis=0, keepdims=True), (8, GROUP))
     remote(ends.at[c], ends.at[c], send_small.at[2], ends_sem.at[0], device(dc=1)).start()
-    for k in range(NZ):
-        far = piece(y, x + 2, k)
-        arrived(far, x2_sem.at[k])
-        up_and_down(far, 24 + k)
     arrived(ends.at[1 - c], ends_sem.at[0])
     top = jnp.max(jnp.maximum(ends[0, 0], ends[1, 0]), axis=(0, 1), keepdims=True)
     bottom = jnp.min(jnp.minimum(ends[0, 1], ends[1, 1]), axis=(0, 1), keepdims=True)
@@ -199,12 +219,16 @@
                 result = result * backs[:, at : at + 1]
             dbuf[k, slot] = result.astype(jnp.bfloat16)
 
-    def relay(n, _):
-        xx, zz = x, z
+    def slot_of(n):
+        n = jnp.int32(n)
         order = jnp.where(n < 8, n, jnp.where(n < 24, (n - 8) // 2, n - 24))
         dx = jnp.where(n < 8, 0, jnp.where(n < 24, jnp.where(lax.rem(n, 2) == 0, -1, 1), 2))
         dz = jnp.where(lax.rem(order, 2) == 1, -((order + 1) // 2), order // 2)
-        slot = lax.rem(xx + dx + NX, NX) * NZ + lax.rem(zz + dz + NZ, NZ)
+        return lax.rem(x + dx + NX, NX) * NZ + lax.rem(z + dz + NZ, NZ)
+
+    def relay(n):
+        n = jnp.int32(n)
+        slot = slot_of(n)
         below = abuf.at[lax.rem(y + NY - 1, NY), slot]
         above = abuf.at[lax.rem(y + 1, NY), slot]
         arrived(below, yd_sem.at[n])
@@ -219,6 +243,13 @@
         def _():
             pass_on(above, y2_sem.at[n], dy=-1)
 
+    def take(i):
+        i = jnp.int32(i)
+        group, order = i // NZ, NZ - 1 - lax.rem(i, NZ)
+        dx = jnp.where(group < 2, jnp.where(group == 0, X_ORDER[0], X_ORDER[1]), jnp.where(group == 2, X_ORDER[2], X_ORDER[3]))
+        dz = jnp.where(lax.rem(order, 2) == 1, -((order + 1) // 2), order // 2)
+        slot = lax.rem(x - dx + NX, NX) * NZ + lax.rem(z - dz + NZ, NZ)
+
         @pl.when(active)
         def _():
             @pl.when(slot == me)
@@ -231,44 +262,67 @@
 
             quantize(slot)
 
-        return 0
-
-    lax.fori_loop(0, PLANE, relay, 0)
-
     def last(n, _):
-        order = jnp.where(n < 8, n, jnp.where(n < 24, (n - 8) // 2, n - 24))
-        dx = jnp.where(n < 8, 0, jnp.where(n < 24, jnp.where(lax.rem(n, 2) == 0, -1, 1), 2))
-        dz = jnp.where(lax.rem(order, 2) == 1, -((order + 1) // 2), order // 2)
-        slot = lax.rem(x + dx + NX, NX) * NZ + lax.rem(z + dz + NZ, NZ)
-        arrived(abuf.at[lax.rem(y + 2, NY), slot], y2_sem.at[n])
-        return 0
-
+        arrived(abuf.at[lax.rem(y + 2, NY), slot_of(n)], y2_sem.at[n])
+        return 0
+
+    def multiply(block, k):
+        lhs = abuf[block].reshape(TOKENS, HALF)
+        rhs = dbuf[k, pl.ds(block * SUB, SUB)].reshape(HALF, WIDE)
+        return jnp.dot(lhs, rhs, preferred_element_type=jnp.float32)
+
+    final = lax.rem(y + 2, NY)
+
+    def near(group):
+        block = lax.rem(x - X_ORDER[group] + NX, NX)
+
+        @pl.when(jnp.logical_and(active, block != final))
+        def _():
+            def more(k, _):
+                acc[k] += multiply(block, k)
+                return 0
+
+            lax.fori_loop(0, GRID + 1, more, 0)
+
+    for k in range(NZ):
+        far = piece(y, x + 2, k)
+        arrived(far, x2_sem.at[k])
+        up_and_down(far, 24 + k)
+        relay(2 * k)
+        relay(2 * k + 1)
+        take(k)
+
+    def both(i, _):
+        relay(2 * i)
+        relay(2 * i + 1)
+        take(i)
+        return 0
+
+    def rest(i, _):
+        take(i)
+        return 0
+
+    lax.fori_loop(NZ, 2 * NZ, both, 0)
+    near(0)
+    near(1)
+    lax.fori_loop(2 * NZ, 3 * NZ, rest, 0)
+    near(2)
+    lax.fori_loop(3 * NZ, 4 * NZ, rest, 0)
+    near(3)
     lax.fori_loop(0, PLANE, last, 0)
 
     @pl.when(active)
     def _():
-        def multiply(n, _):
-            block, k = n // (GRID + 1), lax.rem(n, GRID + 1)
-            lhs = abuf[block].reshape(TOKENS, HALF)
-            rhs = dbuf[k, pl.ds(block * SUB, SUB)].reshape(HALF, WIDE)
-            product = jnp.dot(lhs, rhs, preferred_element_type=jnp.float32)
-
-            @pl.when(block == 0)
-            def _():
-                acc[k] = product
-
-            @pl.when(block > 0)
-            def _():
-                acc[k] += product
-
-            return 0
-
-        lax.fori_loop(0, NY * (GRID + 1), multiply, 0)
-        for k in range(GRID):
-            residue = acc[k] - acc[GRID]
+        acc[GRID] += multiply(final, GRID)
+
+        def finish(k, _):
+            residue = acc[k] + multiply(final, k) - acc[GRID]
             part[k, 0] = residue[:, :GROUP]
             part[k, 1] = residue[:, GROUP:]
             remote(part.at[k, 1 - c], other.at[k], send_part.at[0], part_sem.at[k], device(dc=1)).start()
+            return 0
+
+        lax.fori_loop(0, GRID, finish, 0)
         sums = []
         for k in range(GRID):
             arrived(other.at[k], part_sem.at[k])
@@ -339,16 +393,15 @@
         return 0
 
     lax.fori_loop(1, PLANE, hear_final, 0)
-    finaly[y] = jnp.sum(finals[...], axis=0)
-    for dy in range(1, NY):
-        remote(finaly.at[y], finaly.at[y], send_small.at[4], finy_sem.at[y], device(dy=dy)).start()
-    for dy in range(1, NY):
-        there = lax.rem(y + dy, NY)
+    place_yc = 2 * y + c
+    finaly[place_yc] = jnp.sum(finals[...], axis=0)
+    for n in range(1, NY * NC):
+        to = device(dy=n // NC, dc=n % NC)
+        remote(finaly.at[place_yc], finaly.at[place_yc], send_small.at[4], finy_sem.at[place_yc], to).start()
+    for n in range(1, NY * NC):
+        there = 2 * lax.rem(y + n // NC, NY) + lax.rem(c + n % NC, NC)
         arrived(finaly.at[there], finy_sem.at[there])
-    finalc[c] = jnp.sum(finaly[...], axis=0)
-    remote(finalc.at[c], finalc.at[c], send_small.at[4], finc_sem.at[0], device(dc=1)).start()
-    arrived(finalc.at[1 - c], finc_sem.at[0])
-    total = jnp.sum(finalc[0] + finalc[1], axis=1, keepdims=True)
+    total = jnp.sum(jnp.sum(finaly[...], axis=0), axis=1, keepdims=True)
     errors_out[...] = jnp.broadcast_to(total / (TOKENS * F), (8, GROUP))
 
     for j in range(SUB):
@@ -378,7 +431,7 @@
         arrived(finals.at[0], send_small.at[4])
         return 0
 
-    lax.fori_loop(0, PLANE - 1 + NY - 1 + 1, left_final, 0)
+    lax.fori_loop(0, PLANE - 1 + NY * NC - 1, left_final, 0)
 
     def left_piece(n, _):
         arrived(abuf.at[0, 0], send_piece.at[0])
@@ -421,8 +474,7 @@
             pltpu.VMEM((2, 8, GROUP), f32),
             pltpu.VMEM((8, GROUP), f32),
             pltpu.VMEM((PLANE, 8, GROUP), f32),
-            pltpu.VMEM((NY, 8, GROUP), f32),
-            pltpu.VMEM((NC, 8, GROUP), f32),
+            pltpu.VMEM((NY * NC, 8, GROUP), f32),
             dma((5,)),
             dma((1,)),
             dma((1,)),
@@ -442,8 +494,7 @@
             dma((GRID,)),
             dma((2,)),
             dma((PLANE,)),
-            dma((NY,)),
-            dma((1,)),
+            dma((NY * NC,)),
             dma((1,)),
         ],
         compiler_params=pltpu.CompilerParams(

time: 141 us -> 116 us (0.82)
  Pallas kernels: 137 us -> 111 us
    pallas_call x1, Pallas kernels: 137 us -> 111 us  [on_device(): pl.pallas_call(kernel, out_shape=(jax.ShapeDtypeStruct((1, GROUP), f32),...]
where the time goes in v2:
time: 116 us; the launch traced here: 115 us
  Pallas kernels  111 us (96%)
  local copies, waits for them, and re-layouts  3.69 us (3%)
    pallas_call x1, Pallas kernels, on_device(): pl.pallas_call(kernel, out_shape=(jax.ShapeDtypeStruct((1, GROUP), f32),...  111 us
    slice x2, local copies, waits for them, and re-layouts, on_device(): return (own_mean[0], cols[:GRID, :112], errors[:GRID, 0])  2.56 us

profile of v2, /device:TPU:1, one launch (start us, length us, event | category | flops | bytes accessed | tf_op | source)
XLA Modules:
  0.0 115.3 jit_solution(9408273952771684841)
XLA Ops:
  0.6 111.0 %shard_map.49 = (f32[1,128]{1,0:T(1,128)}, f32[8,128]{1,0:T(8,128)}, f32[8,128]{1,0:T(8,128)}) custom-call(bf16[12,2048]{1,0:T(8,128)(2,1)} %act.1, bf16[128,7168]{1,0:T(8,128)(2,1)} %w.1), custom_call_target="tpu_custom_call" | custom-call | tf_op jit(solution)/shard_map/pallas_call | solution.py:453
  111.6 1.3 %slice_reduce_fusion = f32[4]{0:T(128)} fusion(f32[8,128]{1,0:T(8,128)} %get-tuple-element.8), kind=kLoop, calls=%fused_computation | loop fusion | bytes 32 | tf_op jit(solution)/shard_map/slice | solution.py:504
  112.9 1.3 %slice.6 = f32[4,112]{1,0:T(4,128)} slice(f32[8,128]{1,0:T(8,128)} %get-tuple-element.7), slice={[0:4], [0:112]} | slice | bytes 3584 | tf_op jit(solution)/shard_map/slice | solution.py:504
  114.2 1.1 copy.6

commit v3 on v2

--- a/solution.py
+++ b/solution.py
@@ -22,31 +22,29 @@
 SUB = HALF // GROUP
 DP = ("x", "z", "c")
 Z_ORDER = (0, -1, 1, -2, 2, -3, 3, -4)
-X_ORDER = (0, 3, 1, 2)
+X_ORDER = ((2, 0), (3, 1))
 WAVE = (6.579736255173805, -12.987875283620534, 12.207951996649596, -6.691021837978725, 2.380346767313312, -0.5278301996489366)
-EARLY = (
-    (),
-    ((0, -4),),
-    ((0, 3),),
-    ((0, -3),),
-    (),
-    ((0, 2),),
-    ((0, -2),),
-    ((0, 1), (0, -1), (0, 0)),
-)
+FIRST = 6
+REST = NZ - FIRST
 MESH_ID = pl.DeviceIdType.MESH
 
 
 def kernel(
-    act, w, mean_out, cols_out, errors_out,
+    act, w, out,
     swap, abuf, dbuf, acc, part, other, stat, staty, ends, table, inverse, tiles, mine, finals, finaly,
     send_small, send_piece, send_w, send_part,
-    swap_sem, z_sem, xl_sem, xr_sem, x2_sem, yd_sem, yu_sem, y2_sem, w_sem, stat_sem, staty_sem, ends_sem,
+    swap_sem, z_sem, xl_sem, xr_sem, x2_sem, yd_sem, yu_sem, y2_sem, qd_sem, qu_sem, q2_sem, ql_sem, qr_sem, qf_sem, w_sem, stat_sem, staty_sem, ends_sem,
     part_sem, tile_sem, fin_sem, finy_sem, own_sem,
 ):
     x, z, c, y = (lax.axis_index(name) for name in ("x", "z", "c", "y"))
     me = x * NZ + z
-    active = me < ACTIVE
+    def works(chip):
+        return lax.rem(chip, 10) != 1
+
+    def pair_of(chip):
+        return chip - (chip + 8) // 10
+
+    active = works(me)
 
     def device(dx=0, dz=0, dc=0, dy=0):
         return {
@@ -87,6 +85,7 @@
             act.at[:, lanes(2 * j + 1 - c)], swap.at[j], send_small.at[0], swap_sem.at[j], device(dc=1)
         ).start()
     here = c == 0
+    out[...] = jnp.zeros((16, GROUP), jnp.float32)
     for j in range(SUB):
         arrived(swap.at[j], swap_sem.at[j])
         own = act[:, lanes(2 * j + c)].astype(jnp.float32)
@@ -102,8 +101,8 @@
 
     lax.fori_loop(1, PLANE, send_stat, 0)
 
-    def columns_of(there):
-        return w.at[:, pl.ds(pl.multiple_of(there * WIDE, WIDE), WIDE)]
+    def columns_of(pair):
+        return w.at[:, pl.ds(pl.multiple_of(pair * WIDE, WIDE), WIDE)]
 
     def index_of(to):
         return to["x"] * NZ + to["z"]
@@ -112,9 +111,9 @@
         to = device(dx, dz)
         there = index_of(to)
 
-        @pl.when(there < ACTIVE)
-        def _():
-            columns = columns_of(there)
+        @pl.when(works(there))
+        def _():
+            columns = columns_of(pair_of(there))
             if dx == 0 and dz == 0:
                 pltpu.make_async_copy(columns, dbuf.at[GRID, me], own_sem.at[0]).start()
             else:
@@ -133,51 +132,65 @@
         pass_on(ref, yd_sem.at[n], dy=1)
         pass_on(ref, yu_sem.at[n], dy=-1)
 
-    for k in range(NZ):
-        ref = piece(y, x, k)
-        if k > 0:
-            arrived(ref, z_sem.at[k])
-        if k == 0 or (k % 2 == 1 and k < 7):
-            pass_on(ref, z_sem.at[k + 1 if k == 0 else k + 2], dz=1)
-        if k == 0 or (k % 2 == 0 and k < 6):
-            pass_on(ref, z_sem.at[k + 2], dz=-1)
-        pass_on(ref, xl_sem.at[k], dx=1)
-        pass_on(ref, xr_sem.at[k], dx=-1)
-        up_and_down(ref, k)
-        for item in EARLY[k]:
-            send_weight(*item)
-
     def hear_stat(n, _):
         there = lax.rem(x + n // NZ, NX) * NZ + lax.rem(z + lax.rem(n, NZ), NZ)
         arrived(stat.at[there], stat_sem.at[there])
         return 0
 
-    lax.fori_loop(1, PLANE, hear_stat, 0)
-    staty[y] = jnp.sum(stat[...], axis=0)
-    for dy in range(1, NY):
-        remote(staty.at[y], staty.at[y], send_small.at[1], staty_sem.at[y], device(dy=dy)).start()
+    def left_and_right(ref, m):
+        pass_on(ref, ql_sem.at[m], dx=1)
+        pass_on(ref, qr_sem.at[m], dx=-1)
 
     for k in range(NZ):
+        ref = piece(y, x, k)
+        if k == 0:
+            for n in range(1, NZ):
+                pass_on(ref, z_sem.at[n], dz=-Z_ORDER[n])
+        else:
+            arrived(ref, z_sem.at[k])
+        if k < FIRST:
+            pass_on(ref, xl_sem.at[k], dx=1)
+            pass_on(ref, xr_sem.at[k], dx=-1)
+            up_and_down(ref, k)
+        else:
+            pass_on(ref, qd_sem.at[k - FIRST], dy=1)
+            pass_on(ref, qu_sem.at[k - FIRST], dy=-1)
+            left_and_right(ref, k - FIRST)
+        for dx in X_ORDER[0]:
+            send_weight(dx, Z_ORDER[7 - k])
+        if k == 2:
+            lax.fori_loop(1, PLANE, hear_stat, 0)
+            staty[y] = jnp.sum(stat[...], axis=0)
+            for dy in range(1, NY):
+                remote(staty.at[y], staty.at[y], send_small.at[1], staty_sem.at[y], device(dy=dy)).start()
+
+    for k in range(FIRST):
         left, right = piece(y, x - 1, k), piece(y, x + 1, k)
         arrived(left, xl_sem.at[k])
-        if k < 4:
+        if k < FIRST // 2:
             pass_on(left, x2_sem.at[k], dx=1)
-        up_and_down(left, 8 + 2 * k)
+        up_and_down(left, FIRST + 2 * k)
         arrived(right, xr_sem.at[k])
-        if k >= 4:
+        if k >= FIRST // 2:
             pass_on(right, x2_sem.at[k], dx=-1)
-        up_and_down(right, 9 + 2 * k)
-        send_weight(2, Z_ORDER[7 - k])
-    for k in range(NZ):
-        send_weight(3, Z_ORDER[7 - k])
-        send_weight(1, Z_ORDER[7 - k])
+        up_and_down(right, FIRST + 1 + 2 * k)
+    for q in range(REST):
+        below, above = piece(y - 1, x, FIRST + q), piece(y + 1, x, FIRST + q)
+        arrived(below, qd_sem.at[q])
+        if q < REST // 2:
+            pass_on(below, q2_sem.at[q], dy=1)
+        left_and_right(below, REST + 2 * q)
+        arrived(above, qu_sem.at[q])
+        if q >= REST // 2:
+            pass_on(above, q2_sem.at[q], dy=-1)
+        left_and_right(above, REST + 1 + 2 * q)
 
     for dy in range(1, NY):
         there = lax.rem(y + dy, NY)
         arrived(staty.at[there], staty_sem.at[there])
     channel_mean = staty[...].reshape(PLANE, GROUP) / TOKENS + 1e-06
     own_mean = staty[x, pl.ds(z, 1), :] / TOKENS + 1e-06
-    mean_out[...] = own_mean
+    out[8:9, :] = own_mean
     log_mean = jnp.log(channel_mean)
     ends[c, 0] = jnp.broadcast_to(jnp.max(log_mean, axis=0, keepdims=True), (8, GROUP))
     ends[c, 1] = jnp.broadcast_to(jnp.min(log_mean, axis=0, keepdims=True), (8, GROUP))
@@ -221,8 +234,9 @@
 
     def slot_of(n):
         n = jnp.int32(n)
-        order = jnp.where(n < 8, n, jnp.where(n < 24, (n - 8) // 2, n - 24))
-        dx = jnp.where(n < 8, 0, jnp.where(n < 24, jnp.where(lax.rem(n, 2) == 0, -1, 1), 2))
+        order = jnp.where(n < FIRST, n, jnp.where(n < 3 * FIRST, (n - FIRST) // 2, n - 3 * FIRST))
+        beside = jnp.where(lax.rem(n - FIRST + NX * NZ, 2) == 0, -1, 1)
+        dx = jnp.where(n < FIRST, 0, jnp.where(n < 3 * FIRST, beside, 2))
         dz = jnp.where(lax.rem(order, 2) == 1, -((order + 1) // 2), order // 2)
         return lax.rem(x + dx + NX, NX) * NZ + lax.rem(z + dz + NZ, NZ)
 
@@ -245,8 +259,9 @@
 
     def take(i):
         i = jnp.int32(i)
-        group, order = i // NZ, NZ - 1 - lax.rem(i, NZ)
-        dx = jnp.where(group < 2, jnp.where(group == 0, X_ORDER[0], X_ORDER[1]), jnp.where(group == 2, X_ORDER[2], X_ORDER[3]))
+        first, even = i < 2 * NZ, lax.rem(i, 2) == 0
+        order = NZ - 1 - lax.rem(i // 2, NZ)
+        dx = jnp.where(first, jnp.where(even, X_ORDER[0][0], X_ORDER[0][1]), jnp.where(even, X_ORDER[1][0], X_ORDER[1][1]))
         dz = jnp.where(lax.rem(order, 2) == 1, -((order + 1) // 2), order // 2)
         slot = lax.rem(x - dx + NX, NX) * NZ + lax.rem(z - dz + NZ, NZ)
 
@@ -271,58 +286,88 @@
         rhs = dbuf[k, pl.ds(block * SUB, SUB)].reshape(HALF, WIDE)
         return jnp.dot(lhs, rhs, preferred_element_type=jnp.float32)
 
-    final = lax.rem(y + 2, NY)
-
-    def near(group):
-        block = lax.rem(x - X_ORDER[group] + NX, NX)
-
-        @pl.when(jnp.logical_and(active, block != final))
-        def _():
-            def more(k, _):
-                acc[k] += multiply(block, k)
-                return 0
-
-            lax.fori_loop(0, GRID + 1, more, 0)
-
-    for k in range(NZ):
+    def accumulate(block):
+        for k in range(GRID + 1):
+            acc[k] += multiply(block, k)
+
+    later = [(dx, Z_ORDER[7 - k]) for k in range(NZ) for dx in X_ORDER[1]]
+    for k in range(FIRST):
         far = piece(y, x + 2, k)
         arrived(far, x2_sem.at[k])
-        up_and_down(far, 24 + k)
-        relay(2 * k)
-        relay(2 * k + 1)
+        up_and_down(far, 3 * FIRST + k)
+        for n in range(3 * k, 3 * k + 3):
+            relay(n)
+        for item in later[3 * k : 3 * k + 3]:
+            send_weight(*item)
         take(k)
-
-    def both(i, _):
-        relay(2 * i)
-        relay(2 * i + 1)
+    for q in range(REST):
+        across = piece(y + 2, x, FIRST + q)
+        arrived(across, q2_sem.at[q])
+        left_and_right(across, 3 * REST + q)
+        take(FIRST + q)
+
+    def side(m, dx):
+        q = m if m < REST else (m - REST) // 2 if m < 3 * REST else m - 3 * REST
+        dy = 0 if m < REST else (1 if (m - REST) % 2 else -1) if m < 3 * REST else 2
+        return piece(y + dy, x + dx, FIRST + q)
+
+    def beside(m):
+        arrived(side(m, -1), ql_sem.at[m])
+        if m % 2 == 0:
+            pass_on(side(m, -1), qf_sem.at[m], dx=1)
+        arrived(side(m, 1), qr_sem.at[m])
+        if m % 2 == 1:
+            pass_on(side(m, 1), qf_sem.at[m], dx=-1)
+
+    for m in range(2 * REST):
+        beside(m)
+
+    def two(j, _):
+        relay(3 * FIRST + j)
+        take(NZ + j)
+        return 0
+
+    def one(i, _):
         take(i)
         return 0
 
-    def rest(i, _):
-        take(i)
-        return 0
-
-    lax.fori_loop(NZ, 2 * NZ, both, 0)
-    near(0)
-    near(1)
-    lax.fori_loop(2 * NZ, 3 * NZ, rest, 0)
-    near(2)
-    lax.fori_loop(3 * NZ, 4 * NZ, rest, 0)
-    near(3)
-    lax.fori_loop(0, PLANE, last, 0)
+    lax.fori_loop(0, FIRST, two, 0)
+    for m in range(2 * REST, 3 * REST):
+        beside(m)
+    lax.fori_loop(NZ + FIRST, 2 * NZ, one, 0)
+    for m in range(3 * REST, 4 * REST):
+        beside(m)
+    for m in range(3 * REST):
+        arrived(side(m, 2), qf_sem.at[m])
+    opposite = lax.rem(x - y + NX, NX) == 2
+    sooner = lax.rem(jnp.where(opposite, x + 2, x), NX)
+    later_one = lax.rem(jnp.where(opposite, x, x + 2), NX)
 
     @pl.when(active)
     def _():
+        accumulate(sooner)
+
+    lax.fori_loop(2 * NZ, 3 * NZ + 4, one, 0)
+    lax.fori_loop(0, NX * FIRST, last, 0)
+    for m in range(3 * REST, 4 * REST):
+        arrived(side(m, 2), qf_sem.at[m])
+
+    @pl.when(active)
+    def _():
+        accumulate(later_one)
+
+    lax.fori_loop(3 * NZ + 4, 4 * NZ, one, 0)
+    final = lax.rem(x + NX - 1, NX)
+
+    @pl.when(active)
+    def _():
+        accumulate(lax.rem(x + 1, NX))
         acc[GRID] += multiply(final, GRID)
-
-        def finish(k, _):
+        for k in range(GRID):
             residue = acc[k] + multiply(final, k) - acc[GRID]
             part[k, 0] = residue[:, :GROUP]
             part[k, 1] = residue[:, GROUP:]
             remote(part.at[k, 1 - c], other.at[k], send_part.at[0], part_sem.at[k], device(dc=1)).start()
-            return 0
-
-        lax.fori_loop(0, GRID, finish, 0)
         sums = []
         for k in range(GRID):
             arrived(other.at[k], part_sem.at[k])
@@ -334,12 +379,13 @@
     def _():
         mine[...] = jnp.zeros((8, GROUP), jnp.float32)
 
-    tile = 2 * me + c
+    seat = 2 * me + c
+    tile = 2 * pair_of(me) + c
     owner = (tile // 7) * 8 + lax.rem(tile, 7)
 
     def send_tile(to_index, slot):
         to = {"x": to_index // (NZ * NC), "z": lax.rem(to_index // NC, NZ), "c": lax.rem(to_index, NC), "y": y}
-        same = to_index == tile
+        same = to_index == seat
 
         @pl.when(jnp.logical_not(same))
         def _():
@@ -362,11 +408,14 @@
 
     lax.fori_loop(1, PLANE, send_final, 0)
 
-    place = lax.rem(tile, 8)
-    before = (tile // 8) * 7 + place - 1
+    place = lax.rem(seat, 8)
+    before = (seat // 8) * 7 + place - 1
     after = before + 1
 
-    @pl.when(jnp.logical_and(place > 0, before != tile))
+    def from_other(source):
+        return jnp.logical_not(jnp.logical_and(active, source == tile))
+
+    @pl.when(jnp.logical_and(place > 0, from_other(before)))
     def _():
         arrived(tiles.at[0], tile_sem.at[0])
 
@@ -374,7 +423,7 @@
     def _():
         tiles[0] = jnp.zeros((8, GROUP), jnp.float32)
 
-    @pl.when(jnp.logical_and(place < 7, after != tile))
+    @pl.when(jnp.logical_and(place < 7, from_other(after)))
     def _():
         arrived(tiles.at[1], tile_sem.at[1])
 
@@ -385,7 +434,7 @@
     shift = 16 * place
     lane = lax.broadcasted_iota(jnp.int32, (8, GROUP), 1)
     joined = jnp.where(lane < shift, pltpu.roll(tiles[0], shift, 1), pltpu.roll(tiles[1], shift, 1))
-    cols_out[...] = joined / TOKENS
+    out[0:8, :] = joined / TOKENS
 
     def hear_final(n, _):
         there = lax.rem(x + n // NZ, NX) * NZ + lax.rem(z + lax.rem(n, NZ), NZ)
@@ -402,7 +451,9 @@
         there = 2 * lax.rem(y + n // NC, NY) + lax.rem(c + n % NC, NC)
         arrived(finaly.at[there], finy_sem.at[there])
     total = jnp.sum(jnp.sum(finaly[...], axis=0), axis=1, keepdims=True)
-    errors_out[...] = jnp.broadcast_to(total / (TOKENS * F), (8, GROUP))
+    row = lax.broadcasted_iota(jnp.int32, (8, GROUP), 0)
+    spread = jnp.where(row == lane, jnp.broadcast_to(total / (TOKENS * F), (8, GROUP)), 0.0)
+    out[9:10, :] = jnp.sum(spread, axis=0, keepdims=True)
 
     for j in range(SUB):
         arrived(swap.at[j], send_small.at[0])
@@ -416,11 +467,11 @@
 
     @pl.when(active)
     def _():
-        @pl.when(owner != tile)
+        @pl.when(owner != seat)
         def _():
             arrived(mine, send_small.at[3])
 
-        @pl.when(owner + 1 != tile)
+        @pl.when(owner + 1 != seat)
         def _():
             arrived(mine, send_small.at[3])
 
@@ -444,21 +495,23 @@
         return 0
 
     lax.fori_loop(0, jnp.where(active, ACTIVE - 1, ACTIVE), left_weight, 0)
+
+
+def unpack(packed, mean_out, cols_out, errors_out):
+    mean_out[...] = packed[8, :]
+    cols_out[...] = packed[:GRID, : cols_out.shape[1]]
+    errors_out[...] = packed[9, :GRID]
 
 
 def on_device(activations, weight):
     vmem = pl.BlockSpec(memory_space=pltpu.VMEM)
     dma = pltpu.SemaphoreType.DMA
     f32, bf16 = jnp.float32, jnp.bfloat16
-    own_mean, cols, errors = pl.pallas_call(
+    packed = pl.pallas_call(
         kernel,
-        out_shape=(
-            jax.ShapeDtypeStruct((1, GROUP), f32),
-            jax.ShapeDtypeStruct((8, GROUP), f32),
-            jax.ShapeDtypeStruct((8, GROUP), f32),
-        ),
+        out_shape=jax.ShapeDtypeStruct((16, GROUP), f32),
         in_specs=[vmem, pl.BlockSpec(memory_space=pl.ANY)],
-        out_specs=(vmem, vmem, vmem),
+        out_specs=vmem,
         scratch_shapes=[
             pltpu.VMEM((SUB, ROWS // 2, GROUP), bf16),
             pltpu.VMEM((NY, PLANE, ROWS, HALF), bf16),
@@ -484,9 +537,15 @@
             dma((NZ,)),
             dma((NZ,)),
             dma((NZ,)),
-            dma((PLANE,)),
-            dma((PLANE,)),
-            dma((PLANE,)),
+            dma((NX * FIRST,)),
+            dma((NX * FIRST,)),
+            dma((NX * FIRST,)),
+            dma((REST,)),
+            dma((REST,)),
+            dma((REST,)),
+            dma((NY * REST,)),
+            dma((NY * REST,)),
+            dma((NY * REST,)),
             dma((PLANE,)),
             dma((PLANE,)),
             dma((NY,)),
@@ -501,7 +560,16 @@
             collective_id=0, has_side_effects=True, vmem_limit_bytes=60 * 1024 * 1024
         ),
     )(activations, weight)
-    return own_mean[0], cols[:GRID, :112], errors[:GRID, 0]
+    return pl.pallas_call(
+        unpack,
+        out_shape=(
+            jax.ShapeDtypeStruct((GROUP,), f32),
+            jax.ShapeDtypeStruct((GRID, F // (PLANE * NC * NY)), f32),
+            jax.ShapeDtypeStruct((GRID,), f32),
+        ),
+        in_specs=[vmem],
+        out_specs=(vmem, vmem, vmem),
+    )(packed)
 
 
 def solution(mesh):

time: 116 us -> 107 us (0.922)
  Pallas kernels: 111 us -> 107 us
  local copies, waits for them, and re-layouts: 3.69 us -> 0 us
    pallas_call x1 -> x2, Pallas kernels: 111 us -> 107 us  [the longest x1 105 us: on_device(): pl.pallas_call(kernel, out_shape=jax.ShapeDtypeStruct((16, GROUP), f32),...]
    slice x2 -> x0, local copies, waits for them, and re-layouts: 2.56 us -> none  [on_device(): return (own_mean[0], cols[:GRID, :112], errors[:GRID, 0])]
where the time goes in v3:
time: 107 us
  Pallas kernels  107 us (100%)
    pallas_call x1, Pallas kernels, on_device(): pl.pallas_call(kernel, out_shape=jax.ShapeDtypeStruct((16, GROUP), f32),...  105 us

profile of v3, /device:TPU:1, one launch (start us, length us, event | category | flops | bytes accessed | tf_op | source)
XLA Modules:
  0.0 107.3 jit_solution(4049342850536298099)
XLA Ops:
  0.6 105.4 %shard_map.49.packed = f32[16,128]{1,0:T(8,128)} custom-call(bf16[12,2048]{1,0:T(8,128)(2,1)} %act.1, bf16[128,7168]{1,0:T(8,128)(2,1)} %w.1), custom_call_target="tpu_custom_call" | custom-call | tf_op jit(solution)/shard_map/pallas_call | solution.py:510
  106.0 1.3 %shard_map.50 = (f32[128]{0:T(128)}, f32[4,112]{1,0:T(4,128)}, f32[4]{0:T(128)}) custom-call(f32[16,128]{1,0:T(8,128)} %shard_map.49.packed), custom_call_target="tpu_custom_call" | custom-call | tf_op jit(solution)/shard_map/pallas_call | solution.py:563

commit v4 on v3

--- a/solution.py
+++ b/solution.py
@@ -31,7 +31,7 @@
 
 def kernel(
     act, w, out,
-    swap, abuf, dbuf, acc, part, other, stat, staty, ends, table, inverse, tiles, mine, finals, finaly,
+    swap, abuf, dbuf, acc, part, other, stat, staty, ends, table, inverse, spread, tiles, mine, finals, finaly,
     send_small, send_piece, send_w, send_part,
     swap_sem, z_sem, xl_sem, xr_sem, x2_sem, yd_sem, yu_sem, y2_sem, qd_sem, qu_sem, q2_sem, ql_sem, qr_sem, qf_sem, w_sem, stat_sem, staty_sem, ends_sem,
     part_sem, tile_sem, fin_sem, finy_sem, own_sem,
@@ -208,29 +208,34 @@
     table[...] = stacked.T
     inverse[...] = (1.0 / stacked).T
 
-    def quantize(slot):
-        weight = dbuf[GRID, slot].astype(jnp.float32)
+
+    def widen(slot):
         factors = pltpu.roll(table[...], GROUP - slot, 1)
         backs = pltpu.roll(inverse[...], GROUP - slot, 1)
-        for k in range(GRID):
-            if k == 0:
-                scaled = weight
-            else:
-                at = (k - 1) * PLANE
-                scaled = weight * factors[:, at : at + 1]
-            step = (jnp.max(jnp.abs(scaled), axis=0, keepdims=True) + 1e-06) * (1.0 / 7.0)
-            value = scaled * (1.0 / step)
-            whole = jnp.round(value)
-            rest = value - whole
-            square = rest * rest
-            wave = jnp.full_like(square, WAVE[-1])
-            for term in WAVE[-2::-1]:
-                wave = wave * square + term
-            level = whole + rest * square * wave
-            result = level * step
-            if k > 0:
-                result = result * backs[:, at : at + 1]
-            dbuf[k, slot] = result.astype(jnp.bfloat16)
+        for k in range(GRID - 1):
+            at = k * PLANE
+            spread[slot, k, 0] = jnp.broadcast_to(factors[:, at : at + 1], (GROUP, GROUP))
+            spread[slot, k, 1] = jnp.broadcast_to(backs[:, at : at + 1], (GROUP, GROUP))
+
+    def quantize(slot):
+        for half in range(WIDE // GROUP):
+            at = slice(half * GROUP, (half + 1) * GROUP)
+            weight = dbuf[GRID, slot, :, at].astype(jnp.float32)
+            for k in range(GRID):
+                scaled = weight if k == 0 else weight * spread[slot, k - 1, 0]
+                step = (jnp.max(jnp.abs(scaled), axis=0, keepdims=True) + 1e-06) * (1.0 / 7.0)
+                value = scaled * (1.0 / step)
+                whole = jnp.round(value)
+                rest = value - whole
+                square = rest * rest
+                wave = jnp.full_like(square, WAVE[-1])
+                for term in WAVE[-2::-1]:
+                    wave = wave * square + term
+                level = whole + rest * square * wave
+                result = level * step
+                if k > 0:
+                    result = result * spread[slot, k - 1, 1]
+                dbuf[k, slot, :, at] = result.astype(jnp.bfloat16)
 
     def slot_of(n):
         n = jnp.int32(n)
@@ -257,16 +262,22 @@
         def _():
             pass_on(above, y2_sem.at[n], dy=-1)
 
-    def take(i):
+    def source(i):
         i = jnp.int32(i)
         first, even = i < 2 * NZ, lax.rem(i, 2) == 0
         order = NZ - 1 - lax.rem(i // 2, NZ)
         dx = jnp.where(first, jnp.where(even, X_ORDER[0][0], X_ORDER[0][1]), jnp.where(even, X_ORDER[1][0], X_ORDER[1][1]))
         dz = jnp.where(lax.rem(order, 2) == 1, -((order + 1) // 2), order // 2)
-        slot = lax.rem(x - dx + NX, NX) * NZ + lax.rem(z - dz + NZ, NZ)
+        return lax.rem(x - dx + NX, NX) * NZ + lax.rem(z - dz + NZ, NZ)
+
+    def take(i, wide=True):
+        slot = source(i)
 
         @pl.when(active)
         def _():
+            if wide:
+                widen(slot)
+
             @pl.when(slot == me)
             def _():
                 pltpu.make_async_copy(dbuf.at[GRID, slot], dbuf.at[GRID, slot], own_sem.at[0]).wait()
@@ -324,19 +335,30 @@
 
     def two(j, _):
         relay(3 * FIRST + j)
+
+        @pl.when(active)
+        def _():
+            def ahead(n, _):
+                widen(source(n))
+                return 0
+
+            lax.fori_loop(2 * NZ + 3 * j, jnp.minimum(2 * NZ + 3 * j + 3, 4 * NZ), ahead, 0)
+
         take(NZ + j)
         return 0
 
     def one(i, _):
-        take(i)
-        return 0
-
-    lax.fori_loop(0, FIRST, two, 0)
+        take(i, False)
+        return 0
+
+    lax.fori_loop(0, FIRST // 2, two, 0)
     for m in range(2 * REST, 3 * REST):
         beside(m)
-    lax.fori_loop(NZ + FIRST, 2 * NZ, one, 0)
+    lax.fori_loop(FIRST // 2, FIRST, two, 0)
     for m in range(3 * REST, 4 * REST):
         beside(m)
+    for i in range(NZ + FIRST, 2 * NZ):
+        take(i)
     for m in range(3 * REST):
         arrived(side(m, 2), qf_sem.at[m])
     opposite = lax.rem(x - y + NX, NX) == 2
@@ -452,8 +474,8 @@
         arrived(finaly.at[there], finy_sem.at[there])
     total = jnp.sum(jnp.sum(finaly[...], axis=0), axis=1, keepdims=True)
     row = lax.broadcasted_iota(jnp.int32, (8, GROUP), 0)
-    spread = jnp.where(row == lane, jnp.broadcast_to(total / (TOKENS * F), (8, GROUP)), 0.0)
-    out[9:10, :] = jnp.sum(spread, axis=0, keepdims=True)
+    placed = jnp.where(row == lane, jnp.broadcast_to(total / (TOKENS * F), (8, GROUP)), 0.0)
+    out[9:10, :] = jnp.sum(placed, axis=0, keepdims=True)
 
     for j in range(SUB):
         arrived(swap.at[j], send_small.at[0])
@@ -524,6 +546,7 @@
             pltpu.VMEM((NC, 2, 8, GROUP), f32),
             pltpu.VMEM((GROUP, GROUP), f32),
             pltpu.VMEM((GROUP, GROUP), f32),
+            pltpu.VMEM((PLANE, GRID - 1, 2, GROUP, GROUP), f32),
             pltpu.VMEM((2, 8, GROUP), f32),
             pltpu.VMEM((8, GROUP), f32),
             pltpu.VMEM((PLANE, 8, GROUP), f32),

time: 107 us -> 106 us (level)
  Pallas kernels: 107 us -> 105 us
    pallas_call x1, Pallas kernels: 105 us -> 104 us  [on_device(): pl.pallas_call(kernel, out_shape=jax.ShapeDtypeStruct((16, GROUP), f32),...]
where the time goes in v4:
time: 106 us
  Pallas kernels  105 us (99%)
    pallas_call x1, Pallas kernels, on_device(): pl.pallas_call(kernel, out_shape=jax.ShapeDtypeStruct((16, GROUP), f32),...  104 us

profile of v4, /device:TPU:1, one launch (start us, length us, event | category | flops | bytes accessed | tf_op | source)
XLA Modules:
  0.0 105.9 jit_solution(10319524151991079307)
XLA Ops:
  0.6 103.9 %shard_map.49.packed = f32[16,128]{1,0:T(8,128)} custom-call(bf16[12,2048]{1,0:T(8,128)(2,1)} %act.1, bf16[128,7168]{1,0:T(8,128)(2,1)} %w.1), custom_call_target="tpu_custom_call" | custom-call | tf_op jit(solution)/shard_map/pallas_call | solution.py:532
  104.6 1.3 %shard_map.50 = (f32[128]{0:T(128)}, f32[4,112]{1,0:T(4,128)}, f32[4]{0:T(128)}) custom-call(f32[16,128]{1,0:T(8,128)} %shard_map.49.packed), custom_call_target="tpu_custom_call" | custom-call | tf_op jit(solution)/shard_map/pallas_call | solution.py:586

commit v5 on v4

--- a/solution.py
+++ b/solution.py
@@ -26,6 +26,7 @@
 WAVE = (6.579736255173805, -12.987875283620534, 12.207951996649596, -6.691021837978725, 2.380346767313312, -0.5278301996489366)
 FIRST = 6
 REST = NZ - FIRST
+LATER = (0, 1, 3, 6, 9, 12, 16)
 MESH_ID = pl.DeviceIdType.MESH
 
 
@@ -308,7 +309,7 @@
         up_and_down(far, 3 * FIRST + k)
         for n in range(3 * k, 3 * k + 3):
             relay(n)
-        for item in later[3 * k : 3 * k + 3]:
+        for item in later[LATER[k] : LATER[k + 1]]:
             send_weight(*item)
         take(k)
     for q in range(REST):

time: 106 us -> 105 us (level)
  no operation moved by 1% of the time
where the time goes in v5:
time: 105 us
  Pallas kernels  104 us (99%)
    pallas_call x1, Pallas kernels, on_device(): pl.pallas_call(kernel, out_shape=jax.ShapeDtypeStruct((16, GROUP), f32),...  103 us

profile of v5, /device:TPU:1, one launch (start us, length us, event | category | flops | bytes accessed | tf_op | source)
XLA Modules:
  0.0 104.8 jit_solution(18323368473022776746)
XLA Ops:
  0.6 102.9 %shard_map.49.packed = f32[16,128]{1,0:T(8,128)} custom-call(bf16[12,2048]{1,0:T(8,128)(2,1)} %act.1, bf16[128,7168]{1,0:T(8,128)(2,1)} %w.1), custom_call_target="tpu_custom_call" | custom-call | tf_op jit(solution)/shard_map/pallas_call | solution.py:533
  103.6 1.3 %shard_map.50 = (f32[128]{0:T(128)}, f32[4,112]{1,0:T(4,128)}, f32[4]{0:T(128)}) custom-call(f32[16,128]{1,0:T(8,128)} %shard_map.49.packed), custom_call_target="tpu_custom_call" | custom-call | tf_op jit(solution)/shard_map/pallas_call | solution.py:587
